TPU v7x, 256 devices: a whole 4x4x8 slice. The times are simulated.
256 devices in a mesh: row: 16 (over y_lo, x, core), col: 16 (over z, y_hi).
Axes of the slice: x: 4, y: 4 (y_hi: 2, y_lo: 2; y = y_hi * 2 + y_lo), z: 8, core: 2. Of those that a mesh axis runs over, the one named last changes fastest.
Arguments:
- tokens: bfloat16 [16, 16, 736, 1024], P('row', 'col'), may hold values from -6 to 6
- local_params: bfloat16 [16, 16, 2, 1024, 1024], P('row', 'col'), may hold values from -0.1875 to 0.1875
- outer_params: float32 [2, 16, 16, 16, 4, 1024], P(None, None, 'col', 'row'), may hold values from -0.1875 to 0.1875
- momentum: float32 [2, 16, 16, 16, 4, 1024], P(None, None, 'col', 'row'), may hold values from -0.1875 to 0.1875
- table: int32 [16, 16], replicated, may hold values from 0 to 15, each once within a row
- counts: int32 [16, 16], replicated, may hold values from 64 to 4095
Outputs:
- path_params: bfloat16 [16, 16, 2, 1024, 1024], P('row', 'col')
- outer_out: float32 [2, 16, 16, 16, 4, 1024], P(None, None, 'col', 'row')
- momentum_out: float32 [2, 16, 16, 16, 4, 1024], P(None, None, 'col', 'row')
- hidden_out: bfloat16 [16, 16, 736, 1024], P('row', 'col')
Inputs may be any that keep to these rules, and one draw needn't show every extreme that they name: Each row of the table names every level-two module exactly once.
All inputs are finite; a program needn't handle non-finite values.
Results may differ from a plain program's by a relative error of at most 0.01.
Values may be sent and summed in bfloat16 or wider, within the bound.
No kernel may reach another device: no remote copies, remote signals or barrier semaphores. Data moves between devices by JAX's collectives and lax.ppermute only.
A program may use at most 64 MiB of HBM per device.

v0:
```python
import jax
import jax.numpy as jnp
from jax import lax
from jax.sharding import PartitionSpec as P


def cut_along(shard, dim, count):
    before, after = (shard.shape[:dim], shard.shape[dim + 1 :])
    return jnp.moveaxis(shard.reshape(*before, count, -1, *after), dim, 0)


def sum_at_owner(shard, axis, dim):
    blocks = cut_along(shard, dim, lax.axis_size(axis))
    arrived = lax.all_to_all(blocks, axis, split_axis=0, concat_axis=0, tiled=True)
    return arrived.astype(jnp.float32).sum(axis=0)


def outer_round(scaled, outer, moment, my_row, inverse):
    layers = scaled.shape[0]
    width = scaled.shape[-1]
    n_col = lax.axis_size("col")
    pieces = scaled.reshape(layers, n_col, width // n_col, width)
    arrived = lax.all_to_all(pieces, "col", split_axis=1, concat_axis=1, tiled=True)
    ordered = jnp.take(arrived, inverse, axis=1)
    summed = sum_at_owner(ordered, "row", 2)
    delta = outer - summed
    moment_new = 0.9 * moment + delta
    outer_new = outer - 0.7 * (delta + 0.9 * moment_new)
    whole = lax.all_gather(outer_new.astype(jnp.bfloat16), "row", axis=2, tiled=True)
    chosen = jnp.take(whole, my_row, axis=1)
    returned = lax.all_to_all(chosen, "col", split_axis=1, concat_axis=1, tiled=True)
    return (outer_new, moment_new, returned.reshape(layers, width, width))


def micro_step(tokens_path, params_path):
    state = tokens_path.astype(jnp.float32)
    for layer in range(params_path.shape[0]):
        scale = lax.rsqrt(jnp.mean(state * state, axis=-1, keepdims=True) + 1e-06)
        normed = (state * scale).astype(jnp.bfloat16)
        mixed = jnp.dot(normed, params_path[layer], preferred_element_type=jnp.float32)
        state = state + jax.nn.gelu(mixed, approximate=False)
    return state.astype(jnp.bfloat16)


def on_device(tokens, local_params, outer_params, momentum, table, counts):
    row_index = lax.axis_index("row")
    col_index = lax.axis_index("col")
    n_col = table.shape[1]
    ids = jnp.arange(n_col, dtype=jnp.int32)
    matches = (table[:, :, None] == ids[None, None, :]).astype(jnp.float32)
    totals = jnp.sum(counts.astype(jnp.float32)[:, :, None] * matches, axis=(0, 1))
    my_row = lax.dynamic_index_in_dim(table, row_index, 0, keepdims=False)
    count_row = lax.dynamic_index_in_dim(counts, row_index, 0, keepdims=False)
    my_module = lax.dynamic_index_in_dim(my_row, col_index, 0, keepdims=False)
    my_count = lax.dynamic_index_in_dim(count_row, col_index, 0, keepdims=False)
    share = my_count.astype(jnp.float32) / jnp.sum(totals * (ids == my_module).astype(jnp.float32))
    inverse = jnp.sum(ids[:, None] * (my_row[:, None] == ids[None, :]).astype(jnp.int32), axis=0)
    params = local_params[0, 0]
    layers = params.shape[0]
    width = params.shape[-1]
    scaled = (share * params.astype(jnp.float32)).astype(jnp.bfloat16)
    outer = outer_params.reshape(layers, n_col, -1, width)
    moment = momentum.reshape(layers, n_col, -1, width)
    outer_new, moment_new, returned = outer_round(scaled, outer, moment, my_row, inverse)
    hidden = micro_step(tokens[0, 0], params)
    return (
        returned[None, None],
        outer_new.reshape(outer_params.shape),
        moment_new.reshape(momentum.shape),
        hidden[None, None],
    )


def solution(mesh):
    return jax.shard_map(
        on_device,
        mesh=mesh,
        in_specs=(
            P("row", "col", None, None),
            P("row", "col", None, None, None),
            P(None, None, "col", "row", None, None),
            P(None, None, "col", "row", None, None),
            P(),
            P(),
        ),
        out_specs=(
            P("row", "col", None, None, None),
            P(None, None, "col", "row", None, None),
            P(None, None, "col", "row", None, None),
            P("row", "col", None, None),
        ),
        check_vma=False,
    )
```

profile of v0, /device:TPU:1, one launch (start us, length us, event | category | flops | bytes accessed | tf_op | source)
XLA Modules:
  0.0 381.6 jit_solution(6195041350932074072)
XLA Ops:
  7.2 0.7 convert_element_type.53
  7.9 1.3 dynamic_slice.12
  9.1 1.3 dynamic_slice.13
  10.4 0.8 select_reduce_fusion
  11.9 1.2 fusion.49
  13.9 3.3 multiply_convert_fusion
  17.1 2.5 copy.58
  19.6 11.8 %all-to-all-start = ((bf16[2,16,64,1024]{3,2,0,1:T(8,128)(2,1)}), bf16[2,16,64,1024]{3,2,0,1:T(8,128)(2,1)}, u32[]{:S(2)}, u32[]{:S(2)}) async-start(bf16[2,16,64,1024]{3,2,0,1:T(8,128)(2,1)} %copy.58), calls=%async_computation | async-start | bytes 8388608 | tf_op jit(solution)/shard_map/all_to_all | solution.py:23
  31.4 0.0 all-gather.2.cloned.1.call-start
  31.4 0.7 compare_and_fusion
  32.1 0.1 select_reduce_fusion.1
  32.3 97.6 %all-to-all-done = bf16[2,16,64,1024]{3,2,0,1:T(8,128)(2,1)} async-done(((bf16[2,16,64,1024]{3,2,0,1:T(8,128)(2,1)}), bf16[2,16,64,1024]{3,2,0,1:T(8,128)(2,1)}, u32[]{:S(2)}, u32[]{:S(2)}) %all-to-all-start) | async-done | bytes 4194336 | tf_op jit(solution)/shard_map/all_to_all | solution.py:23
  129.9 5.0 %gather_fusion = bf16[16,2,64,1024]{3,2,1,0:T(8,128)(2,1)} fusion(bf16[2,16,64,1024]{3,2,0,1:T(8,128)(2,1)} %all-to-all-done, s32[1024]{0:T(1024)S(1)} %pad_clamp_fusion.1), kind=kCustom, calls=%fused_computation.clone | custom fusion | bytes 8388672 | tf_op jit(solution)/shard_map/jit(_take)/gather | solution.py:24
  134.9 4.7 %select_bitcast_fusion.1 = bf16[2,16,64,1024]{3,2,0,1:T(8,128)(2,1)} fusion(bf16[16,2,64,1024]{3,2,1,0:T(8,128)(2,1)} %gather_fusion, pred[16]{0:T(512)(128)(4,1)S(1)} %compare_and_fusion.1), kind=kLoop, calls=%fused_computation.8 | loop fusion | flops 2097152 | bytes 8388624 | tf_op jit(solution)/shard_map/jit(_take)/select_n | solution.py:24
  139.6 7.2 %reshape.72 = bf16[2,16,16,4,1024]{4,3,2,0,1:T(4,128)(2,1)} reshape(bf16[2,16,64,1024]{3,2,0,1:T(8,128)(2,1)} %select_bitcast_fusion.1) | data formatting | bytes 8388608 | tf_op jit(solution)/shard_map/reshape | solution.py:9
  146.8 4.6 %copy.93 = bf16[2,16,16,4,1024]{4,3,0,1,2:T(4,128)(2,1)S(1)} copy(bf16[2,16,16,4,1024]{4,3,2,0,1:T(4,128)(2,1)} %reshape.72) | data formatting | bytes 8388608 | tf_op jit(solution)/shard_map/reshape | solution.py:9
  151.3 54.5 %all_to_all.15 = bf16[16,2,16,4,1024]{4,3,1,2,0:T(4,128)(2,1)S(1)} all-to-all(bf16[16,2,16,4,1024]{4,3,1,2,0:T(4,128)(2,1)S(1)} %bitcast.75), channel_id=1, replica_groups=mesh['row'=16,'col'=16] {'row'}, dimensions={0} | all-to-all | bytes 8388608 | tf_op jit(solution)/shard_map/all_to_all | solution.py:14
  205.8 0.0 copy-start.1
  205.8 0.0 copy-start.2
  205.8 2.2 convert_reduce_fusion
  208.1 0.0 copy-done.1
  208.1 0.0 copy-done.2
  208.1 0.6 fusion.47
  208.7 0.9 copy.63
  209.6 0.0 all-gather.2.cloned.1.call-update
  209.7 35.8 %all-gather.2.cloned.1.call-done = bf16[2,16,64,1024]{3,1,0,2:T(8,128)(2,1)} async-done(((bf16[2,16,4,1024]{3,1,0,2:T(8,128)(2,1)}), bf16[2,16,64,1024]{3,1,0,2:T(8,128)(2,1)}) %all-gather.2.cloned.1.call-update) | async-done | bytes 4194320 | tf_op jit(solution)/shard_map/all_gather | solution.py:29
  245.5 6.5 %copy.64 = bf16[2,16,64,1024]{3,2,1,0:T(8,128)(2,1)} copy(bf16[2,16,64,1024]{3,1,0,2:T(8,128)(2,1)} %all-gather.2.cloned.1.call-done) | data formatting | bytes 8388608 | tf_op jit(solution)/shard_map/all_gather | solution.py:29
  252.0 4.9 %gather_fusion.1 = bf16[16,2,64,1024]{3,2,1,0:T(8,128)(2,1)} fusion(bf16[2,16,64,1024]{3,2,1,0:T(8,128)(2,1)} %copy.64, s32[1024]{0:T(1024)S(1)} %pad_clamp_fusion), kind=kCustom, calls=%fused_computation.1.clone | custom fusion | bytes 8388672 | tf_op jit(solution)/shard_map/jit(_take)/gather | solution.py:30
  256.9 4.7 %select_bitcast_fusion = bf16[2,16,64,1024]{3,2,0,1:T(8,128)(2,1)} fusion(bf16[16,2,64,1024]{3,2,1,0:T(8,128)(2,1)} %gather_fusion.1, pred[16]{0:T(512)(128)(4,1)S(1)} %get-tuple-element.25), kind=kLoop, calls=%fused_computation.7 | loop fusion | flops 2097152 | bytes 8388624 | tf_op jit(solution)/shard_map/jit(_take)/select_n | solution.py:30
  261.6 0.0 copy-start.3
  261.6 9.2 %all-to-all-start.2 = ((bf16[2,16,64,1024]{3,2,0,1:T(8,128)(2,1)}), bf16[2,16,64,1024]{3,2,0,1:T(8,128)(2,1)}, u32[]{:S(2)}, u32[]{:S(2)}) async-start(bf16[2,16,64,1024]{3,2,0,1:T(8,128)(2,1)} %select_bitcast_fusion), calls=%async_computation.2 | async-start | bytes 8388608 | tf_op jit(solution)/shard_map/all_to_all | solution.py:31
  270.8 0.0 copy-done.3
  270.8 0.4 fusion.2
  271.2 0.0 copy-start
  271.2 10.1 %multiply_reduce_fusion = (f32[736]{0:T(1024)S(1)}, f32[736,1024]{1,0:T(8,128)S(1)}) fusion(bf16[1,1,2,1024,1024]{4,3,2,1,0:T(8,128)(2,1)} %param.9, bf16[1,1,736,1024]{3,2,1,0:T(8,128)(2,1)S(1)} %copy-done.3, f32[736]{0:T(1024)S(1)} %add_rsqrt_fusion.1), kind=kOutput, calls=%fused_computation.35 | convolution fusion | flops 1597013248 | bytes 8133504 | tf_op jit(solution)/shard_map/dot_general | solution.py:40
  281.3 0.0 copy-done
  281.3 9.4 %fusion.36 = bf16[1,1,736,1024]{3,2,1,0:T(8,128)(2,1)} fusion(f32[736,1024]{1,0:T(8,128)S(1)} %get-tuple-element.30, bf16[1,1,2,1024,1024]{4,3,2,1,0:T(8,128)(2,1)S(1)} %copy-done, f32[736]{0:T(1024)S(1)} %add_rsqrt_fusion), kind=kOutput, calls=%fused_computation.62 | convolution fusion | flops 1594753024 | bytes 9637888 | tf_op jit(solution)/shard_map/dot_general | solution.py:40
  290.7 0.7 fusion.48
  291.4 0.8 copy.68
  292.2 0.8 copy.69
  293.0 76.8 %all-to-all-done.2 = bf16[2,16,64,1024]{3,2,0,1:T(8,128)(2,1)} async-done(((bf16[2,16,64,1024]{3,2,0,1:T(8,128)(2,1)}), bf16[2,16,64,1024]{3,2,0,1:T(8,128)(2,1)}, u32[]{:S(2)}, u32[]{:S(2)}) %all-to-all-start.2) | async-done | bytes 4194336 | tf_op jit(solution)/shard_map/all_to_all | solution.py:31
  369.8 4.9 %copy.65 = bf16[2,16,64,1024]{3,2,1,0:T(8,128)(2,1)} copy(bf16[2,16,64,1024]{3,2,0,1:T(8,128)(2,1)} %all-to-all-done.2) | data formatting | bytes 8388608 | tf_op jit(solution)/shard_map/all_to_all | solution.py:31
  (7 shorter events, 0.0 us)
Async XLA Ops:
  19.6 110.3 %all-to-all-start = ((bf16[2,16,64,1024]{3,2,0,1:T(8,128)(2,1)}), bf16[2,16,64,1024]{3,2,0,1:T(8,128)(2,1)}, u32[]{:S(2)}, u32[]{:S(2)}) async-start(bf16[2,16,64,1024]{3,2,0,1:T(8,128)(2,1)} %copy.58), calls=%async_computation | async-start | bytes 8388608 | tf_op jit(solution)/shard_map/all_to_all | solution.py:23
  31.4 214.1 %all-gather.2.cloned.1.call-start = ((), (), s32[]{:S(2)}) async-start(), calls=%async_computation.3 | async-start | bytes 4456448 | tf_op jit(solution)/shard_map/all_gather | solution.py:29
  205.8 2.3 copy-start.1
  205.8 2.3 copy-start.2
  261.6 9.3 %copy-start.3 = (bf16[1,1,736,1024]{3,2,1,0:T(8,128)(2,1)S(1)}, bf16[1,1,736,1024]{3,2,1,0:T(8,128)(2,1)}, u32[]{:S(2)}) copy-start(bf16[1,1,736,1024]{3,2,1,0:T(8,128)(2,1)} %param.8) | copy-start | bytes 4521988
  261.6 108.2 %all-to-all-start.2 = ((bf16[2,16,64,1024]{3,2,0,1:T(8,128)(2,1)}), bf16[2,16,64,1024]{3,2,0,1:T(8,128)(2,1)}, u32[]{:S(2)}, u32[]{:S(2)}) async-start(bf16[2,16,64,1024]{3,2,0,1:T(8,128)(2,1)} %select_bitcast_fusion), calls=%async_computation.2 | async-start | bytes 8388608 | tf_op jit(solution)/shard_map/all_to_all | solution.py:31
  271.2 10.1 %copy-start = (bf16[1,1,2,1024,1024]{4,3,2,1,0:T(8,128)(2,1)S(1)}, bf16[1,1,2,1024,1024]{4,3,2,1,0:T(8,128)(2,1)}, u32[]{:S(2)}) copy-start(bf16[1,1,2,1024,1024]{4,3,2,1,0:T(8,128)(2,1)} %param.9) | copy-start | bytes 12582916
Sparse Core Ops, SparseCore 0:
  209.7 35.6 all-gather.1
where the time goes:
time: 382 us
  waiting for transfers between devices  210 us (55%)
  blocking collectives  54.5 us (14%)
  local copies, waits for them, and re-layouts  40.7 us (11%)
  starting transfers between devices  21.1 us (6%)
  other arithmetic  20.2 us (5%)
  matrix products  19.5 us (5%)
  between operations  15.5 us (4%)
    all_to_all x1, waiting for transfers between devices, outer_round(): lax.all_to_all(pieces, 'col', split_axis=1, concat_axis=1, tiled=True)  97.6 us
    all_to_all x1, waiting for transfers between devices, outer_round(): lax.all_to_all(chosen, 'col', split_axis=1, concat_axis=1, tiled=True)  76.8 us
    all_to_all x1, blocking collectives, sum_at_owner(): lax.all_to_all(blocks, axis, split_axis=0, concat_axis=0, tiled=True)  54.5 us
    all_gather x1, waiting for transfers between devices, outer_round(): lax.all_gather(outer_new.astype(jnp.bfloat16), 'row', axis=2, tiled=True)  35.8 us
    dot_general x2, matrix products, micro_step(): jnp.dot(normed, params_path[layer], preferred_element_type=jnp.float32)  19.5 us
    all_to_all x1, starting transfers between devices, outer_round(): lax.all_to_all(pieces, 'col', split_axis=1, concat_axis=1, tiled=True)  11.8 us
    reshape x2, local copies, waits for them, and re-layouts, cut_along(): return jnp.moveaxis(shard.reshape(*before, count, -1, *after), dim, 0)  11.8 us
    all_to_all x1, starting transfers between devices, outer_round(): lax.all_to_all(chosen, 'col', split_axis=1, concat_axis=1, tiled=True)  9.24 us
  transfers between devices with their start and end apart: 3, of which 3 were waited for; matrix products, arithmetic and copies ran while one was open for 6% of the time, Pallas kernels for 0%

commit v1 on v0

--- a/solution.py
+++ b/solution.py
@@ -2,6 +2,11 @@
 import jax.numpy as jnp
 from jax import lax
 from jax.sharding import PartitionSpec as P
+
+
+def gather_blocks(value, axis, d):
+    blocks = lax.all_gather(value, axis)
+    return jnp.concatenate(blocks, axis=d)
 
 
 def cut_along(shard, dim, count):
@@ -26,7 +31,7 @@
     delta = outer - summed
     moment_new = 0.9 * moment + delta
     outer_new = outer - 0.7 * (delta + 0.9 * moment_new)
-    whole = lax.all_gather(outer_new.astype(jnp.bfloat16), "row", axis=2, tiled=True)
+    whole = gather_blocks(outer_new.astype(jnp.bfloat16), "row", 2)
     chosen = jnp.take(whole, my_row, axis=1)
     returned = lax.all_to_all(chosen, "col", split_axis=1, concat_axis=1, tiled=True)
     return (outer_new, moment_new, returned.reshape(layers, width, width))

time: 382 us -> 383 us (level)
    reshape x0 -> x1, local copies, waits for them, and re-layouts: none -> 4.34 us  [gather_blocks(): return jnp.concatenate(blocks, axis=d)]
    all_gather x1, local copies, waits for them, and re-layouts: 6.52 us -> 2.63 us  [gather_blocks(): blocks = lax.all_gather(value, axis)]
where the time goes in v1:
time: 383 us; the launch traced here: 382 us
  waiting for transfers between devices  210 us (55%)
  blocking collectives  54.5 us (14%)
  local copies, waits for them, and re-layouts  41.1 us (11%)
  starting transfers between devices  21.1 us (6%)
  other arithmetic  20.2 us (5%)
  matrix products  19.5 us (5%)
  between operations  15.5 us (4%)
    all_to_all x1, waiting for transfers between devices, outer_round(): lax.all_to_all(pieces, 'col', split_axis=1, concat_axis=1, tiled=True)  97.6 us
    all_to_all x1, waiting for transfers between devices, outer_round(): lax.all_to_all(chosen, 'col', split_axis=1, concat_axis=1, tiled=True)  76.7 us
    all_to_all x1, blocking collectives, sum_at_owner(): lax.all_to_all(blocks, axis, split_axis=0, concat_axis=0, tiled=True)  54.5 us
    all_gather x1, waiting for transfers between devices, gather_blocks(): blocks = lax.all_gather(value, axis)  35.8 us
    dot_general x2, matrix products, micro_step(): jnp.dot(normed, params_path[layer], preferred_element_type=jnp.float32)  19.5 us
    all_to_all x1, starting transfers between devices, outer_round(): lax.all_to_all(pieces, 'col', split_axis=1, concat_axis=1, tiled=True)  11.8 us
    reshape x2, local copies, waits for them, and re-layouts, cut_along(): return jnp.moveaxis(shard.reshape(*before, count, -1, *after), dim, 0)  11.8 us
    all_to_all x1, starting transfers between devices, outer_round(): lax.all_to_all(chosen, 'col', split_axis=1, concat_axis=1, tiled=True)  9.24 us
  transfers between devices with their start and end apart: 3, of which 3 were waited for; matrix products, arithmetic and copies ran while one was open for 6% of the time, Pallas kernels for 0%

profile of v1, /device:TPU:1, one launch (start us, length us, event | category | flops | bytes accessed | tf_op | source)
XLA Modules:
  0.0 382.0 jit_solution(12276511717874717873)
XLA Ops:
  7.2 0.7 convert_element_type.60
  7.9 1.3 dynamic_slice.12
  9.1 1.3 dynamic_slice.13
  10.4 0.8 select_reduce_fusion
  11.9 1.2 fusion.49
  13.9 3.3 multiply_convert_fusion
  17.1 2.5 copy.80
  19.6 11.8 %all-to-all-start = ((bf16[2,16,64,1024]{3,2,0,1:T(8,128)(2,1)}), bf16[2,16,64,1024]{3,2,0,1:T(8,128)(2,1)}, u32[]{:S(2)}, u32[]{:S(2)}) async-start(bf16[2,16,64,1024]{3,2,0,1:T(8,128)(2,1)} %copy.80), calls=%async_computation | async-start | bytes 8388608 | tf_op jit(solution)/shard_map/all_to_all | solution.py:28
  31.4 0.0 all-gather.2.cloned.1.call-start
  31.4 0.7 compare_and_fusion
  32.1 0.1 select_reduce_fusion.1
  32.3 97.6 %all-to-all-done = bf16[2,16,64,1024]{3,2,0,1:T(8,128)(2,1)} async-done(((bf16[2,16,64,1024]{3,2,0,1:T(8,128)(2,1)}), bf16[2,16,64,1024]{3,2,0,1:T(8,128)(2,1)}, u32[]{:S(2)}, u32[]{:S(2)}) %all-to-all-start) | async-done | bytes 4194336 | tf_op jit(solution)/shard_map/all_to_all | solution.py:28
  129.9 5.0 %gather_fusion = bf16[16,2,64,1024]{3,2,1,0:T(8,128)(2,1)} fusion(bf16[2,16,64,1024]{3,2,0,1:T(8,128)(2,1)} %all-to-all-done, s32[1024]{0:T(1024)S(1)} %pad_clamp_fusion.1), kind=kCustom, calls=%fused_computation.clone | custom fusion | bytes 8388672 | tf_op jit(solution)/shard_map/jit(_take)/gather | solution.py:29
  134.9 4.7 %select_bitcast_fusion.1 = bf16[2,16,64,1024]{3,2,0,1:T(8,128)(2,1)} fusion(bf16[16,2,64,1024]{3,2,1,0:T(8,128)(2,1)} %gather_fusion, pred[16]{0:T(512)(128)(4,1)S(1)} %compare_and_fusion.1), kind=kLoop, calls=%fused_computation.8 | loop fusion | flops 2097152 | bytes 8388624 | tf_op jit(solution)/shard_map/jit(_take)/select_n | solution.py:29
  139.6 7.2 %reshape.126 = bf16[2,16,16,4,1024]{4,3,2,0,1:T(4,128)(2,1)} reshape(bf16[2,16,64,1024]{3,2,0,1:T(8,128)(2,1)} %select_bitcast_fusion.1) | data formatting | bytes 8388608 | tf_op jit(solution)/shard_map/reshape | solution.py:14
  146.8 4.6 %copy.116 = bf16[2,16,16,4,1024]{4,3,0,1,2:T(4,128)(2,1)S(1)} copy(bf16[2,16,16,4,1024]{4,3,2,0,1:T(4,128)(2,1)} %reshape.126) | data formatting | bytes 8388608 | tf_op jit(solution)/shard_map/reshape | solution.py:14
  151.3 54.5 %all_to_all.15 = bf16[16,2,16,4,1024]{4,3,1,2,0:T(4,128)(2,1)S(1)} all-to-all(bf16[16,2,16,4,1024]{4,3,1,2,0:T(4,128)(2,1)S(1)} %bitcast.79), channel_id=1, replica_groups=mesh['row'=16,'col'=16] {'row'}, dimensions={0} | all-to-all | bytes 8388608 | tf_op jit(solution)/shard_map/all_to_all | solution.py:19
  205.8 0.0 copy-start.1
  205.8 0.0 copy-start.2
  205.8 2.2 convert_reduce_fusion
  208.1 0.0 copy-done.1
  208.1 0.0 copy-done.2
  208.1 0.6 fusion.47
  208.7 0.9 copy.85
  209.6 0.0 all-gather.2.cloned.1.call-update
  209.7 35.8 %all-gather.2.cloned.1.call-done = bf16[16,2,16,4,1024]{4,2,3,1,0:T(8,128)(2,1)} async-done(((bf16[1,2,16,4,1024]{4,2,3,1,0:T(8,128)(2,1)}), bf16[16,2,16,4,1024]{4,2,3,1,0:T(8,128)(2,1)}) %all-gather.2.cloned.1.call-update) | async-done | bytes 4194320 | tf_op jit(solution)/shard_map/all_gather | solution.py:8
  245.5 2.6 copy.86
  248.1 4.3 %copy.87 = bf16[2,16,64,1024]{3,2,1,0:T(8,128)(2,1)} copy(bf16[2,16,64,1024]{3,1,2,0:T(8,128)(2,1)S(1)} %bitcast.80) | data formatting | bytes 8388608 | tf_op jit(solution)/shard_map/reshape | solution.py:9
  252.4 4.9 %gather_fusion.1 = bf16[16,2,64,1024]{3,2,1,0:T(8,128)(2,1)} fusion(bf16[2,16,64,1024]{3,2,1,0:T(8,128)(2,1)} %copy.87, s32[1024]{0:T(1024)S(1)} %pad_clamp_fusion), kind=kCustom, calls=%fused_computation.1.clone | custom fusion | bytes 8388672 | tf_op jit(solution)/shard_map/jit(_take)/gather | solution.py:35
  257.4 4.7 %select_bitcast_fusion = bf16[2,16,64,1024]{3,2,0,1:T(8,128)(2,1)} fusion(bf16[16,2,64,1024]{3,2,1,0:T(8,128)(2,1)} %gather_fusion.1, pred[16]{0:T(512)(128)(4,1)S(1)} %get-tuple-element.33), kind=kLoop, calls=%fused_computation.7 | loop fusion | flops 2097152 | bytes 8388624 | tf_op jit(solution)/shard_map/jit(_take)/select_n | solution.py:35
  262.0 0.0 copy-start.3
  262.0 9.2 %all-to-all-start.2 = ((bf16[2,16,64,1024]{3,2,0,1:T(8,128)(2,1)}), bf16[2,16,64,1024]{3,2,0,1:T(8,128)(2,1)}, u32[]{:S(2)}, u32[]{:S(2)}) async-start(bf16[2,16,64,1024]{3,2,0,1:T(8,128)(2,1)} %select_bitcast_fusion), calls=%async_computation.2 | async-start | bytes 8388608 | tf_op jit(solution)/shard_map/all_to_all | solution.py:36
  271.3 0.0 copy-done.3
  271.3 0.4 fusion.2
  271.7 0.0 copy-start
  271.7 10.1 %multiply_reduce_fusion = (f32[736]{0:T(1024)S(1)}, f32[736,1024]{1,0:T(8,128)S(1)}) fusion(bf16[1,1,2,1024,1024]{4,3,2,1,0:T(8,128)(2,1)} %param.9, bf16[1,1,736,1024]{3,2,1,0:T(8,128)(2,1)S(1)} %copy-done.3, f32[736]{0:T(1024)S(1)} %add_rsqrt_fusion.1), kind=kOutput, calls=%fused_computation.35 | convolution fusion | flops 1597013248 | bytes 8133504 | tf_op jit(solution)/shard_map/dot_general | solution.py:45
  281.7 0.0 copy-done
  281.7 9.4 %fusion.36 = bf16[1,1,736,1024]{3,2,1,0:T(8,128)(2,1)} fusion(f32[736,1024]{1,0:T(8,128)S(1)} %get-tuple-element.38, bf16[1,1,2,1024,1024]{4,3,2,1,0:T(8,128)(2,1)S(1)} %copy-done, f32[736]{0:T(1024)S(1)} %add_rsqrt_fusion), kind=kOutput, calls=%fused_computation.62 | convolution fusion | flops 1594753024 | bytes 9637888 | tf_op jit(solution)/shard_map/dot_general | solution.py:45
  291.2 0.7 fusion.48
  291.8 0.8 copy.91
  292.7 0.8 copy.92
  293.5 76.7 %all-to-all-done.2 = bf16[2,16,64,1024]{3,2,0,1:T(8,128)(2,1)} async-done(((bf16[2,16,64,1024]{3,2,0,1:T(8,128)(2,1)}), bf16[2,16,64,1024]{3,2,0,1:T(8,128)(2,1)}, u32[]{:S(2)}, u32[]{:S(2)}) %all-to-all-start.2) | async-done | bytes 4194336 | tf_op jit(solution)/shard_map/all_to_all | solution.py:36
  370.3 4.9 %copy.88 = bf16[2,16,64,1024]{3,2,1,0:T(8,128)(2,1)} copy(bf16[2,16,64,1024]{3,2,0,1:T(8,128)(2,1)} %all-to-all-done.2) | data formatting | bytes 8388608 | tf_op jit(solution)/shard_map/all_to_all | solution.py:36
  (7 shorter events, 0.0 us)
Async XLA Ops:
  19.6 110.3 %all-to-all-start = ((bf16[2,16,64,1024]{3,2,0,1:T(8,128)(2,1)}), bf16[2,16,64,1024]{3,2,0,1:T(8,128)(2,1)}, u32[]{:S(2)}, u32[]{:S(2)}) async-start(bf16[2,16,64,1024]{3,2,0,1:T(8,128)(2,1)} %copy.80), calls=%async_computation | async-start | bytes 8388608 | tf_op jit(solution)/shard_map/all_to_all | solution.py:28
  31.4 214.1 %all-gather.2.cloned.1.call-start = ((), (), s32[]{:S(2)}) async-start(), calls=%async_computation.3 | async-start | bytes 4456448 | tf_op jit(solution)/shard_map/all_gather | solution.py:8
  205.8 2.3 copy-start.1
  205.8 2.3 copy-start.2
  262.0 9.3 %copy-start.3 = (bf16[1,1,736,1024]{3,2,1,0:T(8,128)(2,1)S(1)}, bf16[1,1,736,1024]{3,2,1,0:T(8,128)(2,1)}, u32[]{:S(2)}) copy-start(bf16[1,1,736,1024]{3,2,1,0:T(8,128)(2,1)} %param.8) | copy-start | bytes 4521988
  262.0 108.2 %all-to-all-start.2 = ((bf16[2,16,64,1024]{3,2,0,1:T(8,128)(2,1)}), bf16[2,16,64,1024]{3,2,0,1:T(8,128)(2,1)}, u32[]{:S(2)}, u32[]{:S(2)}) async-start(bf16[2,16,64,1024]{3,2,0,1:T(8,128)(2,1)} %select_bitcast_fusion), calls=%async_computation.2 | async-start | bytes 8388608 | tf_op jit(solution)/shard_map/all_to_all | solution.py:36
  271.7 10.1 %copy-start = (bf16[1,1,2,1024,1024]{4,3,2,1,0:T(8,128)(2,1)S(1)}, bf16[1,1,2,1024,1024]{4,3,2,1,0:T(8,128)(2,1)}, u32[]{:S(2)}) copy-start(bf16[1,1,2,1024,1024]{4,3,2,1,0:T(8,128)(2,1)} %param.9) | copy-start | bytes 12582916
Sparse Core Ops, SparseCore 0:
  209.7 35.6 all-gather.1
